TPU v7x, 32 devices: a whole 2x2x4 slice. The times are simulated.
32 devices in a mesh: section: 4 (over z), dp: 2 (over x), tensor: 4 (over y, core).
Axes of the slice: x: 2, y: 2, z: 4, core: 2. Of those that a mesh axis runs over, the one named last changes fastest.
Arguments:
- hidden: bfloat16 [64, 16384], P(('section', 'dp'), 'tensor'), may hold values from -100 to 100
- norm_gain: float32 [16384], replicated, may hold values from 0.5 to 1.5
- head_weight: bfloat16 [8192, 16384], P(('section', 'dp', 'tensor')), may hold values from -100 to 100
- token_ids: int32 [64], P(('section', 'dp')), may hold values from 0 to 8191
- resp_len: int32 [8, 2], P(('section', 'dp')), may hold values from 1 to 4, 6 in all within a row
- group_of: int32 [8, 2], P(('section', 'dp')), may hold values from 0 to 7
- loss_mask: int32 [64], P(('section', 'dp', 'tensor')), may hold values 0 or 1
- old_logp: float32 [64], P(('section', 'dp', 'tensor')), may hold values from -30 to 0
- ref_logp: float32 [64], P(('section', 'dp', 'tensor')), may hold values from -30 to 0
- advantage: float32 [64], P(('section', 'dp', 'tensor')), may hold values from -30 to 30
Outputs:
- token_logp: float32 [64], P(('section', 'dp', 'tensor'))
- group_loss: float32 [8], replicated
- group_count: float32 [8], replicated
Inputs may be any that keep to these rules, and one draw needn't show every extreme that they name: `resp_len`: the response lengths of the 2 sequences of each shard sum to exactly 6.
All inputs are finite; a program needn't handle non-finite values. No bound on the sum of `loss_mask` on one device may be relied on, other than what follows from the above.
Results may differ from a plain program's by a relative error of at most 0.0003.
The roundings to bfloat16 on the way count: a program that leaves them out, or rounds other values in their place, can miss the bound.
Values may be sent and summed in bfloat16 or wider, within the bound.
A program may use at most 128 MiB of HBM per device.

v0:
```python
import jax
import jax.numpy as jnp
from jax import lax
from jax.sharding import PartitionSpec as P

D = 16384
GROUPS = 8


epsilon = 1e-05
clip_range = 0.2
kl_weight = 0.1
log_clamp = 20.0


def combined_all(part, axis, combine):
    gathered = jax.tree.map(lambda a: lax.all_gather(a, axis), part)

    def take(source):
        return jax.tree.map(lambda a: lax.dynamic_index_in_dim(a, source, 0, False), gathered)

    return lax.fori_loop(
        1, lax.axis_size(axis), lambda source, state: combine(state, take(source)), take(0)
    )


def token_loss(logprob, old_logp, ref_logp, advantage, weight):
    ratios = jnp.exp(logprob - old_logp)
    clipped = jnp.clip(ratios, 1.0 - clip_range, 1.0 + clip_range)
    surrogate = jnp.minimum(ratios * advantage, clipped * advantage)
    log_gap = jnp.clip(ref_logp - logprob, -log_clamp, log_clamp)
    penalty = jnp.exp(log_gap) - log_gap - 1.0
    return (kl_weight * penalty - surrogate) * weight


def layout(lengths, row_count):
    local_row = jnp.arange(row_count, dtype=jnp.int32)
    seq_count = lengths.shape[0]
    window = row_count // seq_count
    seq_num = local_row // window
    within = local_row % window
    member = seq_num[:, None] == jnp.arange(seq_count, dtype=jnp.int32)[None, :]
    length_row = jnp.sum(jnp.where(member, lengths[None, :], 0), axis=1)
    before = jnp.cumsum(lengths) - lengths
    offset = jnp.sum(jnp.where(member, before[None, :], 0), axis=1)
    is_live = within >= window - length_row
    live_rank = offset + within - (window - length_row)
    return (member, is_live, live_rank)


def local(
    hidden,
    norm_gain,
    head_weight,
    token_ids,
    resp_len,
    group_of,
    loss_mask,
    old_logp,
    ref_logp,
    advantage,
):
    row_count = hidden.shape[0]
    member, is_live, live_rank = layout(resp_len[0], row_count)
    width_part = hidden.shape[1]
    tensor_idx = lax.axis_index("tensor")
    gain_part = lax.dynamic_slice_in_dim(norm_gain, tensor_idx * width_part, width_part)
    values = hidden.astype(jnp.float32)
    square_sum = lax.psum(jnp.sum(values * values, axis=1), "tensor")
    mean_square = square_sum / D
    outgoing = (values * lax.rsqrt(mean_square + epsilon)[:, None] * gain_part[None, :]).astype(
        jnp.bfloat16
    )
    gathered = lax.all_gather(outgoing, "tensor", axis=1, tiled=True)
    vocab_rows = head_weight.shape[0]
    columns = lax.axis_index(("section", "dp", "tensor")) * vocab_rows + jnp.arange(
        vocab_rows, dtype=jnp.int32
    )
    piece_rows = lax.all_gather(gathered, ("section", "dp"), axis=0, tiled=True)
    piece_ids = lax.all_gather(token_ids, ("section", "dp"), axis=0, tiled=True)
    logits = jnp.einsum("rd,vd->rv", piece_rows, head_weight, preferred_element_type=jnp.float32)
    row_max = jnp.max(logits, axis=1)
    totals = jnp.sum(jnp.exp(logits - row_max[:, None]), axis=1)
    chosen = jnp.sum(jnp.where(piece_ids[:, None] == columns[None, :], logits, 0.0), axis=1)
    stats = (row_max, totals, chosen)

    def combine(earlier, later):
        new_max = jnp.maximum(earlier[0], later[0])
        totals = earlier[1] * jnp.exp(earlier[0] - new_max) + later[1] * jnp.exp(later[0] - new_max)
        return (new_max, totals, earlier[2] + later[2])

    row_max, totals, chosen = combined_all(stats, ("section", "dp", "tensor"), combine)
    log_total = row_max + jnp.log(totals)
    own_count = loss_mask.shape[0]
    own_start = tensor_idx * own_count
    own_live = lax.dynamic_slice_in_dim(is_live, own_start, own_count)
    own_member = lax.dynamic_slice_in_dim(member, own_start, own_count, 0)
    shard_idx = lax.axis_index(("section", "dp"))
    lookup = shard_idx * row_count + own_start + jnp.arange(own_count, dtype=jnp.int32)
    logprob = chosen[lookup] - log_total[lookup]
    token_logp = jnp.where(own_live, logprob, 0.0)
    weight = own_live.astype(jnp.float32) * loss_mask.astype(jnp.float32)
    losses = token_loss(logprob, old_logp, ref_logp, advantage, weight)
    own_group = jnp.sum(jnp.where(own_member, group_of[0][None, :], 0), axis=1)
    group_hit = (own_group[:, None] == jnp.arange(GROUPS, dtype=jnp.int32)[None, :]).astype(
        jnp.float32
    )
    group_loss, group_count = lax.psum(
        (
            jnp.sum(group_hit * losses[:, None], axis=0),
            jnp.sum(group_hit * weight[:, None], axis=0),
        ),
        ("section", "dp", "tensor"),
    )
    return (token_logp, group_loss, group_count)


def solution(mesh):
    return jax.shard_map(
        local,
        mesh=mesh,
        in_specs=(
            P(("section", "dp"), "tensor"),
            P(),
            P(("section", "dp", "tensor"), None),
            P(("section", "dp")),
            P(("section", "dp"), None),
            P(("section", "dp"), None),
            P(("section", "dp", "tensor")),
            P(("section", "dp", "tensor")),
            P(("section", "dp", "tensor")),
            P(("section", "dp", "tensor")),
        ),
        out_specs=(P(("section", "dp", "tensor")), P(), P()),
        check_vma=False,
    )
```

profile of v0, /device:TPU:0, one launch (start us, length us, event | category | flops | bytes accessed | tf_op | source)
XLA Modules:
  0.0 171.9 jit_solution(11519364338927570524)
XLA Ops:
  7.2 0.0 copy-start.3
  7.2 0.0 copy-start.1
  7.2 0.0 copy-start.2
  7.2 0.0 copy-start
  7.2 0.0 all-gather.5.cloned.1.call-start
  7.3 1.0 fusion.7
  8.2 8.4 %psum.21 = f32[8]{0:T(128)S(1)} all-reduce(f32[8]{0:T(128)S(1)} %fusion.7), channel_id=1, replica_groups=mesh['section'=4,'dp'=2,'tensor'=4] {'tensor'}, use_global_device_ids=true, to_apply=%region_2.3 | all-reduce | flops 8 | bytes 64 | tf_op jit(solution)/shard_map/psum | solution.py:69
  16.6 0.7 dynamic_slice.50
  17.4 0.9 fusion.9
  18.3 6.2 %all_gather.27 = bf16[8,16384]{1,0:T(8,128)(2,1)} all-gather(bf16[8,4096]{1,0:T(8,128)(2,1)S(1)} %fusion.9), channel_id=1, replica_groups=mesh['section'=4,'dp'=2,'tensor'=4] {'tensor'}, dimensions={1}, use_global_device_ids=true | all-gather | bytes 327680 | tf_op jit(solution)/shard_map/all_gather | solution.py:74
  24.5 0.0 all-gather.5.cloned.1.call-update
  24.6 1.2 dynamic-slice
  26.5 0.9 dynamic-update-slice.2
  27.3 11.8 %all-reduce.2 = s32[64]{0:T(128)S(1)} all-reduce(s32[64]{0:T(128)S(1)} %dynamic-update-slice.2), channel_id=1, replica_groups=mesh['section'=4,'dp'=2,'tensor'=4] {'section','dp'}, use_global_device_ids=true, to_apply=%add.2 | all-reduce | flops 64 | bytes 512
  39.2 0.1 iota_compare_fusion
  39.3 0.8 fusion.10
  40.0 0.8 select_reduce_fusion.1
  40.9 33.2 %all-gather.5.cloned.1.call-done = bf16[64,16384]{1,0:T(8,128)(2,1)} async-done(((bf16[8,16384]{1,0:T(8,128)(2,1)}), bf16[64,16384]{1,0:T(8,128)(2,1)}) %all-gather.5.cloned.1.call-update) | async-done | bytes 2097168 | tf_op jit(solution)/shard_map/all_gather | solution.py:79
  74.1 6.8 %fusion.18 = (f32[64]{0:T(128)S(1)}, f32[64,256]{1,0:T(8,128)S(1)}) fusion(bf16[64,16384]{1,0:T(8,128)(2,1)} %all-gather.5.cloned.1.call-done, bf16[256,16384]{1,0:T(8,128)(2,1)} %param.14), kind=kOutput, calls=%fused_computation.45 | convolution fusion | flops 536887232 | bytes 10551552 | tf_op jit(solution)/shard_map/rd,vd->rv/dot_general | solution.py:81
  80.9 0.3 dynamic-update-slice
  81.2 0.2 select_reduce_fusion
  81.4 0.3 dynamic-update-slice.3
  81.7 0.3 dynamic-update-slice.1
  82.0 39.5 %all-reduce.5 = (f32[2048]{0:T(1024)S(1)}, f32[2048]{0:T(1024)S(1)}, f32[2048]{0:T(1024)S(1)}) all-reduce(f32[2048]{0:T(1024)S(1)} %dynamic-update-slice, f32[2048]{0:T(1024)S(1)} %dynamic-update-slice.1, f32[2048]{0:T(1024)S(1)} %dynamic-update-slice.3), channel_id=2, replica_groups=mesh['section'=4,'dp'=2,'tensor'=4] {'section','dp','tensor'}, use_global_device_ids=true, to_apply=%add | all-reduce | flops 6144 | bytes 49152
  121.4 0.1 reshape.62
  121.5 0.1 reshape.63
  121.6 0.1 reshape.64
  121.7 1.4 while.19
  123.1 0.6 gather_fusion.1
  123.8 0.6 gather_fusion
  124.4 0.0 copy-done.3
  124.4 0.0 copy-done.1
  124.4 0.0 copy-done.2
  124.4 0.0 copy-done
  124.4 0.6 fusion.15
  125.0 0.1 select_reduce_fusion.2
  125.1 40.0 %all-reduce.4 = (f32[8]{0:T(128)}, f32[8]{0:T(128)}) all-reduce(f32[8]{0:T(128)S(1)} %get-tuple-element.187, f32[8]{0:T(128)S(1)} %get-tuple-element.186), channel_id=1, replica_groups=mesh['section'=4,'dp'=2,'tensor'=4] {'section','dp','tensor'}, use_global_device_ids=true, to_apply=%region_10.11 | all-reduce | flops 16 | bytes 128 | tf_op jit(solution)/shard_map/psum | solution.py:108
  (45 shorter events, 0.9 us)
Async XLA Ops:
  7.2 117.2 %copy-start.3 = (s32[2]{0:T(128)S(1)}, s32[2]{0:T(128)}, u32[]{:S(2)}) copy-start(s32[2]{0:T(128)} %param.18) | copy-start | bytes 28
  7.2 117.2 %copy-start.1 = (f32[2]{0:T(128)S(1)}, f32[2]{0:T(128)}, u32[]{:S(2)}) copy-start(f32[2]{0:T(128)} %param.19) | copy-start | bytes 28
  7.2 117.2 %copy-start.2 = (f32[2]{0:T(128)S(1)}, f32[2]{0:T(128)}, u32[]{:S(2)}) copy-start(f32[2]{0:T(128)} %param.20) | copy-start | bytes 28
  7.2 117.2 %copy-start = (f32[2]{0:T(128)S(1)}, f32[2]{0:T(128)}, u32[]{:S(2)}) copy-start(f32[2]{0:T(128)} %param.21) | copy-start | bytes 28
  7.2 66.9 %all-gather.5.cloned.1.call-start = ((), (), s32[]{:S(2)}) async-start(), calls=%async_computation | async-start | bytes 2359296 | tf_op jit(solution)/shard_map/all_gather | solution.py:79
Sparse Core Ops, SparseCore 0:
  24.7 49.4 all-gather.4
where the time goes:
time: 172 us
  blocking collectives  106 us (62%)
  waiting for transfers between devices  33.3 us (19%)
  between operations  14.8 us (9%)
  matrix products  6.78 us (4%)
  other arithmetic  5.37 us (3%)
  local copies, waits for them, and re-layouts  5.15 us (3%)
    unnamed x2, blocking collectives  51.3 us
    psum x1, blocking collectives, local(): lax.psum((jnp.sum(group_hit * losses[:, None], axis=0), jnp.sum(group_hit...  40 us
    all_gather x1, waiting for transfers between devices, local(): piece_rows = lax.all_gather(gathered, ('section', 'dp'), axis=0, tiled=True)  33.2 us
    psum x1, blocking collectives, local(): square_sum = lax.psum(jnp.sum(values * values, axis=1), 'tensor')  8.39 us
    dot_general x1, matrix products, local(): jnp.einsum('rd,vd->rv', piece_rows, head_weight, preferred_element_type=j...  6.78 us
    all_gather x1, blocking collectives, local(): gathered = lax.all_gather(outgoing, 'tensor', axis=1, tiled=True)  6.23 us
  transfers between devices with their start and end apart: 1, of which 1 were waited for; matrix products, arithmetic and copies ran while one was open for 2% of the time, Pallas kernels for 0%

commit v1 on v0

v1 whole, which is shorter than its diff:
```python
import functools

import jax
import jax.numpy as jnp
from jax import lax
from jax.experimental import pallas as pl
from jax.experimental.pallas import tpu as pltpu
from jax.sharding import PartitionSpec as P

GROUPS = 8
LANES = 128
MESH = pl.DeviceIdType.MESH
F32 = jnp.float32

epsilon = 1e-05
clip_range = 0.2
kl_weight = 0.1
log_clamp = 20.0


def token_loss(logprob, old_logp, ref_logp, advantage, weight):
    ratios = jnp.exp(logprob - old_logp)
    clipped = jnp.clip(ratios, 1.0 - clip_range, 1.0 + clip_range)
    surrogate = jnp.minimum(ratios * advantage, clipped * advantage)
    log_gap = jnp.clip(ref_logp - logprob, -log_clamp, log_clamp)
    penalty = jnp.exp(log_gap) - log_gap - 1.0
    return (kl_weight * penalty - surrogate) * weight


def pick(index, table):
    value = jnp.int32(table[0])
    for j in range(1, len(table)):
        value = jnp.where(index == j, jnp.int32(table[j]), value)
    return value


def kernel(
    sizes,
    hidden,
    gain,
    weight,
    token_ids,
    resp_len,
    group_of,
    loss_mask,
    old_logp,
    ref_logp,
    advantage,
    out_logp,
    out_loss,
    out_count,
    held,
    normed,
    head,
    gain_v,
    logits,
    meta_z,
    meta_x,
    meta_y,
    meta_c,
    stats,
    send_sem,
    recv_sem,
    meta_send,
    meta_recv,
    stat_send,
    stat_recv,
    local_sem,
):
    S, X, T = sizes
    C = 2
    Y = T // C
    N = S * X * T
    z, x, t = (lax.axis_index(a) for a in ("section", "dp", "tensor"))
    y, c = t // C, t % C
    rows, width = hidden.shape
    half = width // 2
    depth = width * T
    tokens = S * X * rows
    vocab = weight.shape[0]
    own_count = loss_mask.shape[0]
    me = (z * X + x) * T + t

    hidden_in = pltpu.make_async_copy(hidden, held.at[z, x, t], local_sem.at[0])
    hidden_in.start()
    gain_in = pltpu.make_async_copy(gain, gain_v, local_sem.at[1])
    gain_in.start()
    head_in = pltpu.make_async_copy(weight, head, local_sem.at[2])
    head_in.start()

    z_at = [z] + [lax.rem(z + d, S) for d in range(1, S)]
    x_at = [x] + [lax.rem(x + d, X) for d in range(1, X)]
    t_at = [t] + [lax.rem(t + d, T) for d in range(1, T)]
    y_at = [y] + [lax.rem(y + d, Y) for d in range(1, Y)]
    others = [
        (dz, dx, dt)
        for dz in range(S)
        for dx in range(X)
        for dt in range(T)
        if dz or dx or dt
    ]

    barrier = pltpu.get_barrier_semaphore()
    for dz, dx, dt in others:
        pl.semaphore_signal(
            barrier,
            inc=1,
            device_id={"section": z_at[dz], "dp": x_at[dx], "tensor": t_at[dt]},
            device_id_type=MESH,
        )

    lane = lax.broadcasted_iota(jnp.int32, (8, LANES * pl.cdiv(tokens, LANES)), 1)
    line = lax.broadcasted_iota(jnp.int32, lane.shape, 0)
    window = rows // resp_len.shape[1]
    own_start = (z * X + x) * rows + t * own_count
    meta = jnp.zeros(lane.shape, F32)
    for j in range(own_count):
        row = t * own_count + j
        within = row % window
        live = jnp.where(within >= window - resp_len[0, row // window], 1.0, 0.0)
        facts = (
            old_logp[j],
            ref_logp[j],
            advantage[j],
            live * loss_mask[j].astype(F32),
            group_of[0, row // window].astype(F32),
            token_ids[row].astype(F32),
            live,
        )
        value = jnp.zeros(lane.shape, F32)
        for i, fact in enumerate(facts):
            value = jnp.where(line == i, fact, value)
        meta = jnp.where(lane == own_start + j, value, meta)
    meta_z[z] = meta

    pl.semaphore_wait(barrier, N - 1)
    hidden_in.wait()

    sends = []

    def block(piece, bz, bx, by, bc):
        return held.at[bz, bx, by * C + bc, :, pl.ds(piece * half, half)]

    def describe(piece, bz, bx, by, bc, target):
        return pltpu.make_async_remote_copy(
            src_ref=block(piece, bz, bx, by, bc),
            dst_ref=block(piece, bz, bx, by, bc),
            send_sem=send_sem.at[len(sends)],
            recv_sem=recv_sem.at[piece, (bz * X + bx) * T + by * C + bc],
            device_id=target,
            device_id_type=MESH,
        )

    def send(piece, bz, bx, by, bc, target):
        copy = describe(piece, bz, bx, by, bc, target)
        copy.start()
        sends.append(copy)

    def arrived(piece, bz, bx, by, bc):
        pltpu.make_async_remote_copy(
            src_ref=block(piece, bz, bx, by, bc),
            dst_ref=block(piece, bz, bx, by, bc),
            send_sem=send_sem.at[0],
            recv_sem=recv_sem.at[piece, (bz * X + bx) * T + by * C + bc],
            device_id={"tensor": y * C + (1 - c)},
            device_id_type=MESH,
        ).wait_recv()

    to_x = [{"dp": x_at[d]} for d in range(1, X)]
    to_y = [{"tensor": y_at[d] * C + c} for d in range(1, Y)]
    to_c = [{"tensor": y * C + (1 - c)}]

    near = [sorted(range(S), key=lambda o, j=j: (abs(o - j), o)) for j in range(S)]
    z_near = [pick(z, [near[j][k] for j in range(S)]) for k in range(S)]

    meta_sends = []

    def meta_copy(buf, slot, order, target):
        return pltpu.make_async_remote_copy(
            src_ref=buf.at[slot],
            dst_ref=buf.at[slot],
            send_sem=meta_send.at[order],
            recv_sem=meta_recv.at[order],
            device_id=target,
            device_id_type=MESH,
        )

    def meta_phase(buf, mine, slots, targets, base):
        def put():
            for d, target in enumerate(targets):
                copy = pltpu.make_async_remote_copy(
                    src_ref=buf.at[mine],
                    dst_ref=buf.at[mine],
                    send_sem=meta_send.at[base + d],
                    recv_sem=meta_recv.at[base + d],
                    device_id=target,
                    device_id_type=MESH,
                )
                copy.start()
                meta_sends.append(copy)

        def take(following, slot):
            for d in range(len(targets)):
                meta_copy(buf, slots[-1 - d], base + d, targets[d]).wait_recv()
            following[slot] = jnp.sum(buf[...], axis=0)

        return put, take

    to_z = [{"section": z_at[d]} for d in range(1, S)]
    put_z, take_z = meta_phase(meta_z, z, z_at[1:], to_z, 0)
    put_x, take_x = meta_phase(meta_x, x, x_at[1:], to_x, S)
    put_y, take_y = meta_phase(meta_y, y, y_at[1:], to_y, S + X)
    put_c, take_c = meta_phase(meta_c, c, [1 - c], to_c, S + X + Y)
    errands = [
        put_z,
        lambda: take_z(meta_x, x),
        put_x,
        lambda: take_x(meta_y, y),
        put_y,
        lambda: take_y(meta_c, c),
        put_c,
    ]

    def from_z(bz, first):
        if not first:
            for piece in (0, 1):
                arrived(piece, bz, x, y, c)
        for target in to_x:
            send(0, bz, x, y, c, target)
        for target in to_y:
            send(1, bz, x, y, c, target)
        for target in to_x:
            send(1, bz, x, y, c, target)
        for target in to_y:
            send(0, bz, x, y, c, target)
        for piece in (0, 1):
            send(piece, bz, x, y, c, to_c[0])

    def from_plane(bz):
        for bx in x_at[1:]:
            arrived(0, bz, bx, y, c)
            for target in to_y + to_c:
                send(0, bz, bx, y, c, target)
        for by in y_at[1:]:
            arrived(1, bz, x, by, c)
            for target in to_x + to_c:
                send(1, bz, x, by, c, target)
        for bx in x_at[1:]:
            arrived(1, bz, bx, y, c)
            send(1, bz, bx, y, c, to_c[0])
        for by in y_at[1:]:
            arrived(0, bz, x, by, c)
            send(0, bz, x, by, c, to_c[0])

    def from_corner(bz):
        for bx in x_at[1:]:
            for by in y_at[1:]:
                for piece in (0, 1):
                    arrived(piece, bz, bx, by, c)
                    send(piece, bz, bx, by, c, to_c[0])

    step = min(width, 1024)

    def normalize(bz, first):
        if first:
            gain_in.wait()
        for bx in range(X):
            for by in range(Y):
                for piece in (0, 1):
                    arrived(piece, bz, bx, by, 1 - c)
        for pair in range(X // 2):
            def values(bt, col):
                return jnp.concatenate(
                    [
                        held[bz, 2 * pair + i, bt, :, pl.ds(col, step)].astype(F32)
                        for i in (0, 1)
                    ],
                    axis=0,
                )

            def squares(i, total):
                for bt in range(T):
                    v = values(bt, pl.multiple_of(i * step, step))
                    v = v * v
                    for k in range(step // LANES):
                        total = total + v[:, k * LANES : (k + 1) * LANES]
                return total

            total = lax.fori_loop(
                0, width // step, squares, jnp.zeros((2 * rows, LANES), F32)
            )
            mean_square = jnp.sum(total, axis=1, keepdims=True) / depth
            scale = lax.rsqrt(mean_square + epsilon)

            def write(i, carry):
                for bt in range(T):
                    col = pl.multiple_of(i * step, step)
                    at = pl.multiple_of(bt * width + i * step, step)
                    v = values(bt, col) * scale * gain_v[:, pl.ds(at, step)]
                    normed[bz * (X // 2) + pair, :, pl.ds(at, step)] = v.astype(jnp.bfloat16)
                return carry

            lax.fori_loop(0, width // step, write, 0)

    for bz in z_near[1:]:
        for piece in (0, 1):
            send(piece, z, x, y, c, {"section": bz})
    errands.pop(0)()
    for k in range(S + 3):
        if k < S:
            from_z(z_near[k], k == 0)
        if 0 <= k - 1 < S:
            from_plane(z_near[k - 1])
        if 0 <= k - 2 < S:
            from_corner(z_near[k - 2])
        if errands:
            errands.pop(0)()
        if 0 <= k - 3 < S:
            normalize(z_near[k - 3], k == 3)
    while errands:
        errands.pop(0)()

    head_in.wait()
    chunk = min(depth, 2048)
    logits[...] = jnp.zeros_like(logits)

    def multiply(i, carry):
        at = pl.multiple_of(i * chunk, chunk)
        part = normed[:, :, pl.ds(at, chunk)].reshape(tokens, chunk)
        logits[...] += lax.dot_general(
            head[:, pl.ds(at, chunk)],
            part,
            (((1,), (1,)), ((), ())),
            preferred_element_type=F32,
        )
        return carry

    lax.fori_loop(0, depth // chunk, multiply, 0)

    meta_copy(meta_c, 1 - c, S + X + Y, to_c[0]).wait_recv()
    meta = jnp.sum(meta_c[...], axis=0)
    facts = [meta[i : i + 1, :tokens] for i in range(7)]

    scores = logits[...]
    row_max = jnp.max(scores, axis=0, keepdims=True)
    totals = jnp.sum(jnp.exp(scores - row_max), axis=0, keepdims=True)
    entry = (lax.broadcasted_iota(jnp.int32, scores.shape, 0) + me * vocab).astype(F32)
    chosen = jnp.sum(jnp.where(entry == facts[5], scores, 0.0), axis=0, keepdims=True)
    padded = meta.shape[1]
    if padded > tokens:
        spare = jnp.zeros((1, padded - tokens), F32)
        row_max, totals, chosen = (
            jnp.concatenate([a, spare], axis=1) for a in (row_max, totals, chosen)
        )
    stats[me, :, :padded] = row_max
    stats[me, :, padded : 2 * padded] = totals
    stats[me, :, 2 * padded :] = chosen

    stat_sends = []
    for k, (dz, dx, dt) in enumerate(reversed(others)):
        copy = pltpu.make_async_remote_copy(
            src_ref=stats.at[me],
            dst_ref=stats.at[me],
            send_sem=stat_send.at[k],
            recv_sem=stat_recv.at[me],
            device_id={"section": z_at[dz], "dp": x_at[dx], "tensor": t_at[dt]},
            device_id_type=MESH,
        )
        copy.start()
        stat_sends.append(copy)
    for dz, dx, dt in others:
        source = (z_at[dz] * X + x_at[dx]) * T + t_at[dt]
        pltpu.make_async_remote_copy(
            src_ref=stats.at[source],
            dst_ref=stats.at[source],
            send_sem=stat_send.at[0],
            recv_sem=stat_recv.at[source],
            device_id=to_c[0],
            device_id_type=MESH,
        ).wait_recv()

    maxima = stats[:, :, :tokens]
    row_max = jnp.max(maxima, axis=0)
    totals = jnp.sum(
        stats[:, :, padded : padded + tokens] * jnp.exp(maxima - row_max[None]), axis=0
    )
    chosen = jnp.sum(stats[:, :, 2 * padded : 2 * padded + tokens], axis=0)
    logprob = chosen - (row_max + jnp.log(totals))
    old, ref, adv, counted, group, unused, live = facts
    losses = token_loss(logprob, old, ref, adv, counted)
    shown = jnp.where(live > 0.5, logprob, 0.0)

    def as_row(member, values, count):
        column = jnp.sum(jnp.where(member, values, 0.0), axis=1, keepdims=True)
        diagonal = lax.broadcasted_iota(jnp.int32, (8, LANES), 0) == lax.broadcasted_iota(
            jnp.int32, (8, LANES), 1
        )
        row = jnp.sum(jnp.where(diagonal, column, 0.0), axis=0, keepdims=True)
        return row[:, :count]

    line = lax.broadcasted_iota(jnp.int32, (8, tokens), 0)
    lane = lax.broadcasted_iota(jnp.int32, (8, tokens), 1)
    in_group = group == line.astype(F32)
    out_logp[...] = as_row(lane == own_start + line, shown, own_count)
    out_loss[...] = as_row(in_group, losses, GROUPS)
    out_count[...] = as_row(in_group, counted, GROUPS)

    for copy in sends + meta_sends + stat_sends:
        copy.wait_send()


def local(sizes, hidden, norm_gain, head_weight, *small):
    S, X, T = sizes
    N = S * X * T
    rows, width = hidden.shape
    depth = norm_gain.shape[0]
    vocab = head_weight.shape[0]
    tokens = S * X * rows
    own_count = small[3].shape[0]
    padded = LANES * pl.cdiv(tokens, LANES)
    Y = T // 2
    copies = 2 * (S - 1 + S * (X - 1) + S * X * (Y - 1) + S * X * Y)
    meta_count = S + X + Y + 2
    anywhere = pl.BlockSpec(memory_space=pl.ANY)
    smem = pl.BlockSpec(memory_space=pltpu.SMEM)
    vmem = pl.BlockSpec(memory_space=pltpu.VMEM)
    dma = pltpu.SemaphoreType.DMA
    logp, loss, count = pl.pallas_call(
        functools.partial(kernel, sizes),
        out_shape=(
            jax.ShapeDtypeStruct((1, own_count), F32),
            jax.ShapeDtypeStruct((1, GROUPS), F32),
            jax.ShapeDtypeStruct((1, GROUPS), F32),
        ),
        in_specs=[anywhere] * 3 + [smem] * 7,
        out_specs=(vmem, vmem, vmem),
        scratch_shapes=[
            pltpu.VMEM((S, X, T, rows, width), jnp.bfloat16),
            pltpu.VMEM((tokens // (2 * rows), 2 * rows, depth), jnp.bfloat16),
            pltpu.VMEM((vocab, depth), jnp.bfloat16),
            pltpu.VMEM((1, depth), F32),
            pltpu.VMEM((vocab, tokens), F32),
            pltpu.VMEM((S, 8, padded), F32),
            pltpu.VMEM((X, 8, padded), F32),
            pltpu.VMEM((Y, 8, padded), F32),
            pltpu.VMEM((2, 8, padded), F32),
            pltpu.VMEM((N, 1, 3 * padded), F32),
            dma((copies,)),
            dma((2, N)),
            dma((meta_count,)),
            dma((meta_count,)),
            dma((N - 1,)),
            dma((N,)),
            dma((3,)),
        ],
        compiler_params=pltpu.CompilerParams(
            collective_id=0, has_side_effects=True, vmem_limit_bytes=60 * 1024 * 1024
        ),
    )(hidden, norm_gain.reshape(1, depth), head_weight, *small)
    return logp.reshape(own_count), loss.reshape(GROUPS), count.reshape(GROUPS)


def solution(mesh):
    sizes = tuple(mesh.shape[a] for a in ("section", "dp", "tensor"))
    return jax.shard_map(
        functools.partial(local, sizes),
        mesh=mesh,
        in_specs=(
            P(("section", "dp"), "tensor"),
            P(),
            P(("section", "dp", "tensor"), None),
            P(("section", "dp")),
            P(("section", "dp"), None),
            P(("section", "dp"), None),
            P(("section", "dp", "tensor")),
            P(("section", "dp", "tensor")),
            P(("section", "dp", "tensor")),
            P(("section", "dp", "tensor")),
        ),
        out_specs=(P(("section", "dp", "tensor")), P(), P()),
        check_vma=False,
    )
```

time: 172 us -> 42.4 us (0.25)
  blocking collectives: 106 us -> 0 us
  Pallas kernels: 0 us -> 38.2 us
  waiting for transfers between devices: 33.3 us -> 0 us
  between operations: 14.8 us -> 0.64 us
  matrix products: 6.78 us -> 0 us
  other arithmetic: 5.37 us -> 0 us
  local copies, waits for them, and re-layouts: 5.15 us -> 3.42 us
    unnamed x2 -> x0, blocking collectives: 51.3 us -> none
    psum x2 -> x0, blocking collectives: 48.4 us -> none  [the longest x1 40 us: local(): lax.psum((jnp.sum(group_hit * losses[:, None], axis=0), jnp.sum(group_hit...]
    pallas_call x0 -> x1, Pallas kernels: none -> 38.2 us  [local(): pl.pallas_call(functools.partial(kernel, sizes), out_shape=(jax.ShapeDtyp...]
    all_gather x1 -> x0, waiting for transfers between devices: 33.2 us -> none  [local(): piece_rows = lax.all_gather(gathered, ('section', 'dp'), axis=0, tiled=True)]
    dot_general x1 -> x0, matrix products: 6.78 us -> none  [local(): jnp.einsum('rd,vd->rv', piece_rows, head_weight, preferred_element_type=j...]
    all_gather x1 -> x0, blocking collectives: 6.23 us -> none  [local(): gathered = lax.all_gather(outgoing, 'tensor', axis=1, tiled=True)]
    reduce_sum x5 -> x0, other arithmetic: 2.86 us -> none  [the longest x1 0.99 us: local(): square_sum = lax.psum(jnp.sum(values * values, axis=1), 'tensor')]
  transfers between devices with their start and end apart: 1 -> 0, of which waited for: 1 -> 0; matrix products, arithmetic and copies ran while one was open for 2% -> 0% of each run, Pallas kernels for 0% -> 0%
where the time goes in v1:
time: 42.4 us; the launch traced here: 42.2 us
  Pallas kernels  38.2 us (90%)
  local copies, waits for them, and re-layouts  3.42 us (8%)
  between operations  0.64 us (2%)
    pallas_call x1, Pallas kernels, local(): pl.pallas_call(functools.partial(kernel, sizes), out_shape=(jax.ShapeDtyp...  38.2 us
    unnamed x3, local copies, waits for them, and re-layouts  3.42 us

profile of v1, /device:TPU:0, one launch (start us, length us, event | category | flops | bytes accessed | tf_op | source)
XLA Modules:
  0.0 42.2 jit_solution(12425294576053707390)
XLA Ops:
  0.6 38.2 %shard_map.121 = (f32[1,2]{1,0:T(1,128)}, f32[1,8]{1,0:T(1,128)}, f32[1,8]{1,0:T(1,128)}) custom-call(bf16[8,4096]{1,0:T(8,128)(2,1)} %hidden.1, f32[1,16384]{1,0:T(1,128)} %bitcast.4, bf16[256,16384]{1,0:T(8,128)(2,1)} %weight.1, s32[8]{0:T(128)} %token_ids.1, s32[1,2]{1,0:T(1,128)} %resp_len.1, s32[1,2]{1,0:T(1,128)} %group_of.1, s32[2]{0:T(128)} %loss_mask.1, ...), custom_call_target="tpu_custom_call" | custom-call | tf_op jit(solution)/shard_map/pallas_call | solution.py:428
  38.8 1.1 %copy.16 = f32[2]{0:T(128)} copy(f32[2]{0:T(128)} %bitcast.7) | data formatting | bytes 16
  39.9 1.1 %copy.17 = f32[8]{0:T(128)} copy(f32[8]{0:T(128)} %bitcast.6) | data formatting | bytes 64
  41.1 1.2 %copy.18 = f32[8]{0:T(128)} copy(f32[8]{0:T(128)} %bitcast.5) | data formatting | bytes 64

commit v2 on v1

--- a/solution.py
+++ b/solution.py
@@ -46,9 +46,7 @@
     old_logp,
     ref_logp,
     advantage,
-    out_logp,
-    out_loss,
-    out_count,
+    out,
     held,
     normed,
     head,
@@ -101,13 +99,12 @@
     ]
 
     barrier = pltpu.get_barrier_semaphore()
-    for dz, dx, dt in others:
-        pl.semaphore_signal(
-            barrier,
-            inc=1,
-            device_id={"section": z_at[dz], "dp": x_at[dx], "tensor": t_at[dt]},
-            device_id_type=MESH,
-        )
+    to_x = [{"dp": x_at[d]} for d in range(1, X)]
+    to_y = [{"tensor": y_at[d] * C + c} for d in range(1, Y)]
+    to_c = [{"tensor": y * C + (1 - c)}]
+    to_z = [{"section": z_at[d]} for d in range(1, S)]
+    for peer in to_z + to_x + to_y + to_c:
+        pl.semaphore_signal(barrier, inc=1, device_id=peer, device_id_type=MESH)
 
     lane = lax.broadcasted_iota(jnp.int32, (8, LANES * pl.cdiv(tokens, LANES)), 1)
     line = lax.broadcasted_iota(jnp.int32, lane.shape, 0)
@@ -133,7 +130,7 @@
         meta = jnp.where(lane == own_start + j, value, meta)
     meta_z[z] = meta
 
-    pl.semaphore_wait(barrier, N - 1)
+    pl.semaphore_wait(barrier, len(to_z + to_x + to_y + to_c))
     hidden_in.wait()
 
     sends = []
@@ -165,10 +162,6 @@
             device_id={"tensor": y * C + (1 - c)},
             device_id_type=MESH,
         ).wait_recv()
-
-    to_x = [{"dp": x_at[d]} for d in range(1, X)]
-    to_y = [{"tensor": y_at[d] * C + c} for d in range(1, Y)]
-    to_c = [{"tensor": y * C + (1 - c)}]
 
     near = [sorted(range(S), key=lambda o, j=j: (abs(o - j), o)) for j in range(S)]
     z_near = [pick(z, [near[j][k] for j in range(S)]) for k in range(S)]
@@ -206,7 +199,6 @@
 
         return put, take
 
-    to_z = [{"section": z_at[d]} for d in range(1, S)]
     put_z, take_z = meta_phase(meta_z, z, z_at[1:], to_z, 0)
     put_x, take_x = meta_phase(meta_x, x, x_at[1:], to_x, S)
     put_y, take_y = meta_phase(meta_y, y, y_at[1:], to_y, S + X)
@@ -390,23 +382,29 @@
     losses = token_loss(logprob, old, ref, adv, counted)
     shown = jnp.where(live > 0.5, logprob, 0.0)
 
-    def as_row(member, values, count):
+    def as_row(member, values):
         column = jnp.sum(jnp.where(member, values, 0.0), axis=1, keepdims=True)
         diagonal = lax.broadcasted_iota(jnp.int32, (8, LANES), 0) == lax.broadcasted_iota(
             jnp.int32, (8, LANES), 1
         )
-        row = jnp.sum(jnp.where(diagonal, column, 0.0), axis=0, keepdims=True)
-        return row[:, :count]
+        return jnp.sum(jnp.where(diagonal, column, 0.0), axis=0, keepdims=True)
 
     line = lax.broadcasted_iota(jnp.int32, (8, tokens), 0)
     lane = lax.broadcasted_iota(jnp.int32, (8, tokens), 1)
     in_group = group == line.astype(F32)
-    out_logp[...] = as_row(lane == own_start + line, shown, own_count)
-    out_loss[...] = as_row(in_group, losses, GROUPS)
-    out_count[...] = as_row(in_group, counted, GROUPS)
+    out[...] = jnp.zeros_like(out)
+    out[0:1, :] = as_row(lane == own_start + line, shown)
+    out[1:2, :] = as_row(in_group, losses)
+    out[2:3, :] = as_row(in_group, counted)
 
     for copy in sends + meta_sends + stat_sends:
         copy.wait_send()
+
+
+def spread(packed, out_logp, out_loss, out_count):
+    out_logp[...] = packed[0:1, : out_logp.shape[1]]
+    out_loss[...] = packed[1:2, : out_loss.shape[1]]
+    out_count[...] = packed[2:3, : out_count.shape[1]]
 
 
 def local(sizes, hidden, norm_gain, head_weight, *small):
@@ -425,15 +423,11 @@
     smem = pl.BlockSpec(memory_space=pltpu.SMEM)
     vmem = pl.BlockSpec(memory_space=pltpu.VMEM)
     dma = pltpu.SemaphoreType.DMA
-    logp, loss, count = pl.pallas_call(
+    packed = pl.pallas_call(
         functools.partial(kernel, sizes),
-        out_shape=(
-            jax.ShapeDtypeStruct((1, own_count), F32),
-            jax.ShapeDtypeStruct((1, GROUPS), F32),
-            jax.ShapeDtypeStruct((1, GROUPS), F32),
-        ),
+        out_shape=jax.ShapeDtypeStruct((8, LANES), F32),
         in_specs=[anywhere] * 3 + [smem] * 7,
-        out_specs=(vmem, vmem, vmem),
+        out_specs=vmem,
         scratch_shapes=[
             pltpu.VMEM((S, X, T, rows, width), jnp.bfloat16),
             pltpu.VMEM((tokens // (2 * rows), 2 * rows, depth), jnp.bfloat16),
@@ -457,6 +451,16 @@
             collective_id=0, has_side_effects=True, vmem_limit_bytes=60 * 1024 * 1024
         ),
     )(hidden, norm_gain.reshape(1, depth), head_weight, *small)
+    logp, loss, count = pl.pallas_call(
+        spread,
+        out_shape=(
+            jax.ShapeDtypeStruct((1, own_count), F32),
+            jax.ShapeDtypeStruct((1, GROUPS), F32),
+            jax.ShapeDtypeStruct((1, GROUPS), F32),
+        ),
+        in_specs=[vmem],
+        out_specs=(vmem, vmem, vmem),
+    )(packed)
     return logp.reshape(own_count), loss.reshape(GROUPS), count.reshape(GROUPS)
 
 

time: 42.4 us -> 38.4 us (0.906)
  local copies, waits for them, and re-layouts: 3.42 us -> 0 us
  Pallas kernels: 38.2 us -> 37.6 us
    unnamed x3 -> x0, local copies, waits for them, and re-layouts: 3.42 us -> none
    pallas_call x1 -> x2, Pallas kernels: 38.2 us -> 37.6 us  [the longest x1 36.4 us: local(): pl.pallas_call(functools.partial(kernel, sizes), out_shape=jax.ShapeDtype...]
where the time goes in v2:
time: 38.4 us; the launch traced here: 38.2 us
  Pallas kernels  37.6 us (98%)
  between operations  0.64 us (2%)
    pallas_call x1, Pallas kernels, local(): pl.pallas_call(functools.partial(kernel, sizes), out_shape=jax.ShapeDtype...  36.4 us
    pallas_call x1, Pallas kernels, local(): pl.pallas_call(spread, out_shape=(jax.ShapeDtypeStruct((1, own_count), F3...  1.19 us

profile of v2, /device:TPU:0, one launch (start us, length us, event | category | flops | bytes accessed | tf_op | source)
XLA Modules:
  0.0 38.2 jit_solution(18218909639655841635)
XLA Ops:
  0.6 36.4 %shard_map.121.packed = f32[8,128]{1,0:T(8,128)} custom-call(bf16[8,4096]{1,0:T(8,128)(2,1)} %hidden.1, f32[1,16384]{1,0:T(1,128)} %bitcast.4, bf16[256,16384]{1,0:T(8,128)(2,1)} %weight.1, s32[8]{0:T(128)} %token_ids.1, s32[1,2]{1,0:T(1,128)} %resp_len.1, s32[1,2]{1,0:T(1,128)} %group_of.1, s32[2]{0:T(128)} %loss_mask.1, f32[2]{0:T(128)} %old_logp.1, ...), custom_call_target="tpu_custom_call" | custom-call | tf_op jit(solution)/shard_map/pallas_call | solution.py:426
  37.0 1.2 %shard_map.122 = (f32[1,2]{1,0:T(1,128)}, f32[1,8]{1,0:T(1,128)}, f32[1,8]{1,0:T(1,128)}) custom-call(f32[8,128]{1,0:T(8,128)} %shard_map.121.packed), custom_call_target="tpu_custom_call" | custom-call | tf_op jit(solution)/shard_map/pallas_call | solution.py:454

commit v3 on v2

--- a/solution.py
+++ b/solution.py
@@ -64,6 +64,7 @@
     stat_send,
     stat_recv,
     local_sem,
+    *small_s,
 ):
     S, X, T = sizes
     C = 2
@@ -81,6 +82,14 @@
 
     hidden_in = pltpu.make_async_copy(hidden, held.at[z, x, t], local_sem.at[0])
     hidden_in.start()
+    small = (token_ids, resp_len, group_of, loss_mask, old_logp, ref_logp, advantage)
+    small_in = [
+        pltpu.make_async_copy(a, b, local_sem.at[3 + i])
+        for i, (a, b) in enumerate(zip(small, small_s))
+    ]
+    for copy in small_in:
+        copy.start()
+    token_ids, resp_len, group_of, loss_mask, old_logp, ref_logp, advantage = small_s
     gain_in = pltpu.make_async_copy(gain, gain_v, local_sem.at[1])
     gain_in.start()
     head_in = pltpu.make_async_copy(weight, head, local_sem.at[2])
@@ -105,30 +114,6 @@
     to_z = [{"section": z_at[d]} for d in range(1, S)]
     for peer in to_z + to_x + to_y + to_c:
         pl.semaphore_signal(barrier, inc=1, device_id=peer, device_id_type=MESH)
-
-    lane = lax.broadcasted_iota(jnp.int32, (8, LANES * pl.cdiv(tokens, LANES)), 1)
-    line = lax.broadcasted_iota(jnp.int32, lane.shape, 0)
-    window = rows // resp_len.shape[1]
-    own_start = (z * X + x) * rows + t * own_count
-    meta = jnp.zeros(lane.shape, F32)
-    for j in range(own_count):
-        row = t * own_count + j
-        within = row % window
-        live = jnp.where(within >= window - resp_len[0, row // window], 1.0, 0.0)
-        facts = (
-            old_logp[j],
-            ref_logp[j],
-            advantage[j],
-            live * loss_mask[j].astype(F32),
-            group_of[0, row // window].astype(F32),
-            token_ids[row].astype(F32),
-            live,
-        )
-        value = jnp.zeros(lane.shape, F32)
-        for i, fact in enumerate(facts):
-            value = jnp.where(line == i, fact, value)
-        meta = jnp.where(lane == own_start + j, value, meta)
-    meta_z[z] = meta
 
     pl.semaphore_wait(barrier, len(to_z + to_x + to_y + to_c))
     hidden_in.wait()
@@ -297,10 +282,35 @@
     for bz in z_near[1:]:
         for piece in (0, 1):
             send(piece, z, x, y, c, {"section": bz})
-    errands.pop(0)()
     for k in range(S + 3):
         if k < S:
             from_z(z_near[k], k == 0)
+        if k == 0:
+            lane = lax.broadcasted_iota(jnp.int32, (8, LANES * pl.cdiv(tokens, LANES)), 1)
+            line = lax.broadcasted_iota(jnp.int32, lane.shape, 0)
+            window = rows // resp_len.shape[1]
+            own_start = (z * X + x) * rows + t * own_count
+            for copy in small_in:
+                copy.wait()
+            meta = jnp.zeros(lane.shape, F32)
+            for j in range(own_count):
+                row = t * own_count + j
+                within = row % window
+                live = jnp.where(within >= window - resp_len[0, row // window], 1.0, 0.0)
+                facts = (
+                    old_logp[j],
+                    ref_logp[j],
+                    advantage[j],
+                    live * loss_mask[j].astype(F32),
+                    group_of[0, row // window].astype(F32),
+                    token_ids[row].astype(F32),
+                    live,
+                )
+                value = jnp.zeros(lane.shape, F32)
+                for i, fact in enumerate(facts):
+                    value = jnp.where(line == i, fact, value)
+                meta = jnp.where(lane == own_start + j, value, meta)
+            meta_z[z] = meta
         if 0 <= k - 1 < S:
             from_plane(z_near[k - 1])
         if 0 <= k - 2 < S:
@@ -313,7 +323,7 @@
         errands.pop(0)()
 
     head_in.wait()
-    chunk = min(depth, 2048)
+    chunk = min(depth, 8192)
     logits[...] = jnp.zeros_like(logits)
 
     def multiply(i, carry):
@@ -420,13 +430,12 @@
     copies = 2 * (S - 1 + S * (X - 1) + S * X * (Y - 1) + S * X * Y)
     meta_count = S + X + Y + 2
     anywhere = pl.BlockSpec(memory_space=pl.ANY)
-    smem = pl.BlockSpec(memory_space=pltpu.SMEM)
     vmem = pl.BlockSpec(memory_space=pltpu.VMEM)
     dma = pltpu.SemaphoreType.DMA
     packed = pl.pallas_call(
         functools.partial(kernel, sizes),
         out_shape=jax.ShapeDtypeStruct((8, LANES), F32),
-        in_specs=[anywhere] * 3 + [smem] * 7,
+        in_specs=[anywhere] * 10,
         out_specs=vmem,
         scratch_shapes=[
             pltpu.VMEM((S, X, T, rows, width), jnp.bfloat16),
@@ -445,8 +454,9 @@
             dma((meta_count,)),
             dma((N - 1,)),
             dma((N,)),
-            dma((3,)),
-        ],
+            dma((3 + len(small),)),
+        ]
+        + [pltpu.SMEM(a.shape, a.dtype) for a in small],
         compiler_params=pltpu.CompilerParams(
             collective_id=0, has_side_effects=True, vmem_limit_bytes=60 * 1024 * 1024
         ),

time: 38.4 us -> 34.6 us (0.901)
  Pallas kernels: 37.6 us -> 33.8 us
    pallas_call x1, Pallas kernels: 36.4 us -> 32.6 us  [local(): pl.pallas_call(functools.partial(kernel, sizes), out_shape=jax.ShapeDtype...]
where the time goes in v3:
time: 34.6 us; the launch traced here: 34.4 us
  Pallas kernels  33.8 us (98%)
  between operations  0.64 us (2%)
    pallas_call x1, Pallas kernels, local(): pl.pallas_call(functools.partial(kernel, sizes), out_shape=jax.ShapeDtype...  32.6 us
    pallas_call x1, Pallas kernels, local(): pl.pallas_call(spread, out_shape=(jax.ShapeDtypeStruct((1, own_count), F3...  1.19 us

profile of v3, /device:TPU:0, one launch (start us, length us, event | category | flops | bytes accessed | tf_op | source)
XLA Modules:
  0.0 34.4 jit_solution(1803064203419210065)
XLA Ops:
  0.6 32.6 %shard_map.121.packed = f32[8,128]{1,0:T(8,128)} custom-call(bf16[8,4096]{1,0:T(8,128)(2,1)} %hidden.1, f32[1,16384]{1,0:T(1,128)} %bitcast.4, bf16[256,16384]{1,0:T(8,128)(2,1)} %weight.1, s32[8]{0:T(128)} %token_ids.1, s32[1,2]{1,0:T(1,128)} %resp_len.1, s32[1,2]{1,0:T(1,128)} %group_of.1, s32[2]{0:T(128)} %loss_mask.1, f32[2]{0:T(128)} %old_logp.1, ...), custom_call_target="tpu_custom_call" | custom-call | tf_op jit(solution)/shard_map/pallas_call | solution.py:435
  33.3 1.2 %shard_map.122 = (f32[1,2]{1,0:T(1,128)}, f32[1,8]{1,0:T(1,128)}, f32[1,8]{1,0:T(1,128)}) custom-call(f32[8,128]{1,0:T(8,128)} %shard_map.121.packed), custom_call_target="tpu_custom_call" | custom-call | tf_op jit(solution)/shard_map/pallas_call | solution.py:464
